TPU v7x, 32 devices: a whole 2x2x4 slice. The times are simulated.
32 devices in a mesh: dp: 8 (over z, core), ctx: 4 (over y, x).
Axes of the slice: x: 2, y: 2, z: 4, core: 2. Of those that a mesh axis runs over, the one named last changes fastest.
Arguments:
- qkv: bfloat16 [8, 512, 5120], P('dp', 'ctx'), may hold values from -8 to 8
- dest: int32 [8, 8], P('dp'), may hold values from 0 to 7, as said below
- order: int32 [8], replicated, may hold values from 0 to 7, as said below
- lengths: int32 [8, 8], replicated, may hold values from 1 to 256, 512 in all within a row
Outputs:
- attended: bfloat16 [8, 512, 4096], P('dp', 'ctx')
Inputs may be any that keep to these rules, and one draw needn't show every extreme that they name: `dest`: entry [r, s] is r itself, r + 1 or r - 1 (indices modulo 8), and the relation is mutual: if entry [r, s] is t, entry [t, s] is r. For every c below 4: order[2 c] is below 4 and order[2 c + 1] = 7 - order[2 c]; every span appears once.
All inputs are finite; a program needn't handle non-finite values.
Results may differ from a plain program's by a relative error of at most 0.0031.
Values may be sent and summed in bfloat16 or wider, within the bound.
A program may use at most 64 MiB of HBM per device.

v0:
```python
import math
import jax
import jax.numpy as jnp
from jax import lax
from jax.sharding import PartitionSpec as P

QUERY_HEADS = 32
KEY_VALUE_HEADS = 4
HEAD_SIZE = 128
NDOC = 8
QUERIES_PER_KV = 8
MASK_FLOOR = -1e30


def passed_along(array, axis, by):
    devices = lax.axis_size(axis)
    return lax.ppermute(array, axis, [(i, (i + by) % devices) for i in range(devices)])


def slot_layout(order, sources, doc_ends, exchanged_rows):
    slot_count = order.shape[0]
    offsets = jnp.arange(exchanged_rows, dtype=jnp.int32)
    positions = (order[:, None] * exchanged_rows + offsets[None, :]).reshape(
        slot_count * exchanged_rows
    )
    slot_ends = jnp.take(doc_ends, sources, axis=0)
    row_ends = jnp.repeat(slot_ends, exchanged_rows, axis=0)
    counted = jnp.sum((row_ends <= positions[:, None]).astype(jnp.int32), axis=1)
    row_source = jnp.repeat(sources, exchanged_rows)
    documents = row_source * NDOC + counted
    return (positions, documents)


def attend(carried, query_head_rows, key_rows, value_rows, visible):
    running_max, accumulated_sum, weighted_values = carried
    scores = jnp.einsum(
        "hqd,khd->hqk", query_head_rows, key_rows, preferred_element_type=jnp.float32
    ) * (1.0 / math.sqrt(HEAD_SIZE))
    tiled_mask = jnp.tile(visible, (QUERIES_PER_KV, 1))[None]
    scores = jnp.where(tiled_mask, scores, MASK_FLOOR)
    new_max = jnp.maximum(running_max, jnp.max(scores, axis=2, keepdims=True))
    weights = jnp.where(tiled_mask, jnp.exp(scores - new_max), 0.0)
    rescale = jnp.exp(running_max - new_max)
    accumulated_sum = accumulated_sum * rescale + jnp.sum(weights, axis=2, keepdims=True)
    update = jnp.einsum(
        "hqk,khd->hqd", weights.astype(jnp.bfloat16), value_rows, preferred_element_type=jnp.float32
    )
    return (new_max, accumulated_sum, weighted_values * rescale + update)


def keep_state(carried, query_head_rows, key_rows, value_rows, visible):
    return carried


def on_device(qkv, dest, order, lengths):
    dp_index = lax.axis_index("dp")
    dp_count = lax.axis_size("dp")
    ctx_index = lax.axis_index("ctx")
    local_rows = qkv.shape[1]
    exchanged_rows = local_rows // 2
    query_width = QUERY_HEADS * HEAD_SIZE
    below = (dp_index + dp_count - 1) % dp_count
    above = (dp_index + 1) % dp_count
    sources = dest[0]
    doc_ends = jnp.cumsum(lengths, axis=1)
    positions, documents = slot_layout(order, sources, doc_ends, exchanged_rows)
    own_sources = lax.dynamic_slice_in_dim(sources, 2 * ctx_index, 2)
    row_from = jnp.repeat(own_sources, exchanged_rows)[:, None]
    resident = qkv[0]
    from_below = passed_along(resident, "dp", 1)
    from_above = passed_along(resident, "dp", -1)
    settled = jnp.where(
        row_from == below, from_below, jnp.where(row_from == above, from_above, resident)
    )
    query_rows = settled[:, :query_width]
    key_values = settled[:, query_width:]
    own_positions = lax.dynamic_slice_in_dim(positions, ctx_index * local_rows, local_rows).reshape(
        2, exchanged_rows
    )
    own_documents = lax.dynamic_slice_in_dim(documents, ctx_index * local_rows, local_rows).reshape(
        2, exchanged_rows
    )
    query_head_rows = query_rows.reshape(
        2, exchanged_rows, KEY_VALUE_HEADS, QUERIES_PER_KV, HEAD_SIZE
    )
    query_head_rows = jnp.transpose(query_head_rows, (0, 2, 3, 1, 4)).reshape(
        2, KEY_VALUE_HEADS, QUERIES_PER_KV * exchanged_rows, HEAD_SIZE
    )

    def fresh_state():
        return (
            jnp.full(
                (KEY_VALUE_HEADS, QUERIES_PER_KV * exchanged_rows, 1), MASK_FLOOR, jnp.float32
            ),
            jnp.zeros((KEY_VALUE_HEADS, QUERIES_PER_KV * exchanged_rows, 1), jnp.float32),
            jnp.zeros((KEY_VALUE_HEADS, QUERIES_PER_KV * exchanged_rows, HEAD_SIZE), jnp.float32),
        )

    portion = lax.all_gather(key_values, "ctx", axis=0, tiled=True)
    piece_rows = portion.shape[0]
    count_of_blocks = piece_rows // local_rows
    block_list = portion.reshape(count_of_blocks, local_rows, 2, KEY_VALUE_HEADS, HEAD_SIZE)

    def absorb_block(states, inputs):
        block_pairs, block_index = inputs
        first_row = block_index * local_rows
        key_positions = lax.dynamic_slice_in_dim(positions, first_row, local_rows)
        key_documents = lax.dynamic_slice_in_dim(documents, first_row, local_rows)
        key_rows = block_pairs[:, 0]
        value_rows = block_pairs[:, 1]
        updated = []
        for half_index in range(2):
            visible = (key_documents[None, :] == own_documents[half_index][:, None]) & (
                key_positions[None, :] <= own_positions[half_index][:, None]
            )
            updated.append(
                lax.cond(
                    jnp.any(visible),
                    attend,
                    keep_state,
                    states[half_index],
                    query_head_rows[half_index],
                    key_rows,
                    value_rows,
                    visible,
                )
            )
        return ((updated[0], updated[1]), None)

    result, unused = lax.scan(
        absorb_block,
        (fresh_state(), fresh_state()),
        (block_list, jnp.arange(count_of_blocks, dtype=jnp.int32)),
    )
    finished = []
    for half_index in range(2):
        running_max, accumulated_sum, weighted_values = result[half_index]
        normalized_output = (weighted_values / accumulated_sum).reshape(
            KEY_VALUE_HEADS, QUERIES_PER_KV, exchanged_rows, HEAD_SIZE
        )
        finished.append(
            jnp.transpose(normalized_output, (2, 0, 1, 3)).reshape(
                exchanged_rows, QUERY_HEADS * HEAD_SIZE
            )
        )
    attended = jnp.concatenate(finished, axis=0).astype(jnp.bfloat16)
    return attended[None]


def solution(mesh):
    return jax.shard_map(
        on_device,
        mesh=mesh,
        in_specs=(P("dp", "ctx", None), P("dp", None), P(), P()),
        out_specs=P("dp", "ctx", None),
        check_vma=False,
    )
```

profile of v0, /device:TPU:1, one launch (start us, length us, event | category | flops | bytes accessed | tf_op | source)
XLA Modules:
  0.0 125.5 jit_solution(16273775453789031055)
XLA Ops:
  6.5 2.7 %collective-permute-start = (bf16[128,5120]{1,0:T(8,128)(2,1)}, bf16[128,5120]{1,0:T(8,128)(2,1)S(1)}, u32[]{:S(2)}, u32[]{:S(2)}) collective-permute-start(bf16[128,5120]{1,0:T(8,128)(2,1)} %bitcast.102), channel_id=1, source_target_pairs={{0,4},{4,8},{8,12},{12,16},{16,20},{20,24},{24,28},{28,0},{1,5},{5... | collective-permute-start | bytes 3932168 | tf_op jit(solution)/shard_map/ppermute | solution.py:17
  12.5 23.6 %collective-permute-done = bf16[128,5120]{1,0:T(8,128)(2,1)S(1)} collective-permute-done((bf16[128,5120]{1,0:T(8,128)(2,1)}, bf16[128,5120]{1,0:T(8,128)(2,1)S(1)}, u32[]{:S(2)}, u32[]{:S(2)}) %collective-permute-start) | collective-permute-done | bytes 1310752 | tf_op jit(solution)/shard_map/ppermute | solution.py:17
  36.1 4.0 %collective-permute-done.1 = bf16[128,5120]{1,0:T(8,128)(2,1)} collective-permute-done((bf16[128,5120]{1,0:T(8,128)(2,1)}, bf16[128,5120]{1,0:T(8,128)(2,1)}, u32[]{:S(2)}, u32[]{:S(2)}) %collective-permute-start.1) | collective-permute-done | bytes 1310752 | tf_op jit(solution)/shard_map/ppermute | solution.py:17
  40.0 2.0 %select_select_fusion = bf16[128,5120]{1,0:T(8,128)(2,1)S(1)} fusion(bf16[128,5120]{1,0:T(8,128)(2,1)S(1)} %collective-permute-done, bf16[128,5120]{1,0:T(8,128)(2,1)} %collective-permute-done.1, pred[128]{0:T(512)(128)(4,1)S(1)} %eq.74, pred[128]{0:T(512)(128)(4,1)S(1)} %eq.70, bf16[1,128,5120]{2,1,0:T(8,128)(2,1)} %param.10), kind=kLoop, calls=%fused_computation.43 | loop fusion | flops 1310720 | bytes 5243136 | tf_op jit(solution)/shard_map/jit(_where)/select_n | solution.py:72
  47.4 1.4 %copy.22 = bf16[2,64,4,8,128]{4,1,3,2,0:T(8,128)(2,1)} copy(bf16[2,64,4,8,128]{4,3,2,1,0:T(8,128)(2,1)S(1)} %bitcast.97) | data formatting | bytes 2097152 | tf_op jit(solution)/shard_map/reshape | solution.py:83
  48.8 20.3 %all-gather.2.cloned.1.call-done = bf16[512,1024]{1,0:T(8,128)(2,1)} async-done(((bf16[128,1024]{1,0:T(8,128)(2,1)}), bf16[512,1024]{1,0:T(8,128)(2,1)}) %all-gather.2.cloned.1.call-update) | async-done | bytes 1048592 | tf_op jit(solution)/shard_map/all_gather | solution.py:99
  69.1 1.8 %reshape.165 = bf16[4,128,2,4,128]{4,3,2,1,0:T(4,128)(2,1)S(1)} reshape(bf16[512,1024]{1,0:T(8,128)(2,1)} %all-gather.2.cloned.1.call-done) | data formatting | bytes 2097152 | tf_op jit(solution)/shard_map/reshape | solution.py:102
  72.8 42.2 %while.20 = (s32[]{:T(128)}, f32[4,512,1]{1,0,2:T(4,128)S(1)}, f32[4,512,1]{1,0,2:T(4,128)}, f32[4,512,128]{2,1,0:T(8,128)S(1)}, f32[4,512,1]{1,0,2:T(4,128)S(1)...) while((s32[]{:T(128)}, f32[4,512,1]{1,0,2:T(4,128)S(1)}, ...), condition=%wide.region_13.14_spmd, body=%wide.region_2.13_spmd.sunk | while | flops 274280448 | bytes 14785039 | solution.py:130
  76.8 1.4 %fusion.32 = (pred[]{:T(512)}, pred[64,128]{1,0:T(8,128)(4,1)S(1)}, pred[]{:T(512)}, pred[64,128]{1,0:T(8,128)(4,1)}) fusion(s32[64]{0:T(128)S(1)} %get-tuple-element.331, s32[128]{0:T(128)S(1)} %dynamic_slice.38, s32[64]{0:T(128)S(1)} %get-tuple-element.332, s32[128]{0:T(128)S(1)} %dynamic_slice.39, s32[64]{0:T(128)S(1)} %get-tuple-element.333, ...), kind=kLoop, calls=%fused_computation.64.clone.1 | loop fusion | flops 65534 | bytes 18434 | tf_op jit(solution)/shard_map/while/body/eval_jaxpr/reduce_or | solution.py:118
  79.1 3.9 %conditional.5 = ((f32[4,512,1]{1,0,2:T(4,128)S(1)}, f32[4,512,1]{1,0,2:T(4,128)}, f32[4,512,128]{2,1,0:T(8,128)S(1)})) conditional(s32[]{:T(128)} %convert_element_type.33, (f32[4,512,1]{1,0,2:T(4,128)S(1)}, f32[4,512,1]{1,0,2:T(4,128)}, f32[4,512,128]{2,1,0:T(8,128)S(1)}) %tuple.61, (pred[64,128]{1,0:T(8,128)(4,1)S(1)}, ...), branch_computations={%region_9.9_spmd, %region_10.12_spmd} | conditional | flops 137107456 | bytes 6561824 | solution.py:117
  79.3 1.4 %fusion.26 = (f32[4,512]{1,0:T(4,128)S(1)}, f32[4,512,128]{1,2,0:T(8,128)S(1)}) fusion(bf16[128,4,128]{2,0,1:T(8,128)(2,1)S(1)} %get-tuple-element.115, bf16[2,4,512,128]{3,2,1,0:T(8,128)(2,1)} %get-tuple-element.114, pred[512,128]{0,1:T(8,128)(4,1)S(1)} %copy.20), kind=kOutput, calls=%fused_computation.67 | convolution fusion | flops 67893248 | bytes 1777664 | tf_op jit(solution)/shard_map/while/body/eval_jaxpr/cond/branch_1_fun/hqd,khd->hqk/dot_general | solution.py:36
  80.9 1.3 %bitcast_add_fusion.1 = f32[4,512,1]{1,0,2:T(4,128)} fusion(f32[4,512]{1,0:T(4,128)S(1)} %fusion.13, f32[4,512,1]{1,0,2:T(4,128)} %get-tuple-element.116, f32[4,512,1]{1,0,2:T(4,128)S(1)} %get-tuple-element.112, f32[4,512,1]{1,0,2:T(4,128)S(1)} %get-tuple-element.356), kind=kLoop, calls=%fused_computation.28 | loop fusion | flops 6144 | bytes 40960 | tf_op jit(solution)/shard_map/while/body/eval_jaxpr/cond/branch_1_fun/add | solution.py:44
  83.6 3.3 %conditional.4 = ((f32[4,512,1]{1,0,2:T(4,128)S(1)}, f32[4,512,1]{1,0,2:T(4,128)}, f32[4,512,128]{2,1,0:T(8,128)S(1)})) conditional(s32[]{:T(128)} %convert_element_type.32, (f32[4,512,1]{1,0,2:T(4,128)S(1)}, f32[4,512,1]{1,0,2:T(4,128)}, f32[4,512,128]{2,1,0:T(8,128)S(1)}) %tuple.59, (pred[64,128]{1,0:T(8,128)(4,1)}, ...), branch_computations={%region_4.4_spmd, %region_5.7_spmd} | conditional | flops 137107456 | bytes 6627416 | solution.py:117
  84.5 1.4 %fusion.25 = (f32[4,512]{1,0:T(4,128)S(1)}, f32[4,512,128]{1,2,0:T(8,128)S(1)}) fusion(bf16[128,4,128]{2,0,1:T(8,128)(2,1)S(1)} %get-tuple-element.108, bf16[2,4,512,128]{3,2,1,0:T(8,128)(2,1)} %get-tuple-element.107, pred[512,128]{0,1:T(8,128)(4,1)S(1)} %copy.18), kind=kOutput, calls=%fused_computation.66 | convolution fusion | flops 67893248 | bytes 1777664 | tf_op jit(solution)/shard_map/while/body/eval_jaxpr/cond/branch_1_fun/hqd,khd->hqk/dot_general | solution.py:36
  91.0 1.4 %fusion.32 = (pred[]{:T(512)}, pred[64,128]{1,0:T(8,128)(4,1)S(1)}, pred[]{:T(512)}, pred[64,128]{1,0:T(8,128)(4,1)}) fusion(s32[64]{0:T(128)S(1)} %get-tuple-element.331, s32[128]{0:T(128)S(1)} %dynamic_slice.38, s32[64]{0:T(128)S(1)} %get-tuple-element.332, s32[128]{0:T(128)S(1)} %dynamic_slice.39, s32[64]{0:T(128)S(1)} %get-tuple-element.333, ...), kind=kLoop, calls=%fused_computation.64.clone.1 | loop fusion | flops 65534 | bytes 18434 | tf_op jit(solution)/shard_map/while/body/eval_jaxpr/reduce_or | solution.py:118
  93.9 3.3 %conditional.4 = ((f32[4,512,1]{1,0,2:T(4,128)S(1)}, f32[4,512,1]{1,0,2:T(4,128)}, f32[4,512,128]{2,1,0:T(8,128)S(1)})) conditional(s32[]{:T(128)} %convert_element_type.32, (f32[4,512,1]{1,0,2:T(4,128)S(1)}, f32[4,512,1]{1,0,2:T(4,128)}, f32[4,512,128]{2,1,0:T(8,128)S(1)}) %tuple.59, (pred[64,128]{1,0:T(8,128)(4,1)}, ...), branch_computations={%region_4.4_spmd, %region_5.7_spmd} | conditional | flops 137107456 | bytes 6627416 | solution.py:117
  94.8 1.4 %fusion.25 = (f32[4,512]{1,0:T(4,128)S(1)}, f32[4,512,128]{1,2,0:T(8,128)S(1)}) fusion(bf16[128,4,128]{2,0,1:T(8,128)(2,1)S(1)} %get-tuple-element.108, bf16[2,4,512,128]{3,2,1,0:T(8,128)(2,1)} %get-tuple-element.107, pred[512,128]{0,1:T(8,128)(4,1)S(1)} %copy.18), kind=kOutput, calls=%fused_computation.66 | convolution fusion | flops 67893248 | bytes 1777664 | tf_op jit(solution)/shard_map/while/body/eval_jaxpr/cond/branch_1_fun/hqd,khd->hqk/dot_general | solution.py:36
  97.2 1.2 dynamic_slice.37
  101.2 1.4 %fusion.32 = (pred[]{:T(512)}, pred[64,128]{1,0:T(8,128)(4,1)S(1)}, pred[]{:T(512)}, pred[64,128]{1,0:T(8,128)(4,1)}) fusion(s32[64]{0:T(128)S(1)} %get-tuple-element.331, s32[128]{0:T(128)S(1)} %dynamic_slice.38, s32[64]{0:T(128)S(1)} %get-tuple-element.332, s32[128]{0:T(128)S(1)} %dynamic_slice.39, s32[64]{0:T(128)S(1)} %get-tuple-element.333, ...), kind=kLoop, calls=%fused_computation.64.clone.1 | loop fusion | flops 65534 | bytes 18434 | tf_op jit(solution)/shard_map/while/body/eval_jaxpr/reduce_or | solution.py:118
  103.5 3.9 %conditional.5 = ((f32[4,512,1]{1,0,2:T(4,128)S(1)}, f32[4,512,1]{1,0,2:T(4,128)}, f32[4,512,128]{2,1,0:T(8,128)S(1)})) conditional(s32[]{:T(128)} %convert_element_type.33, (f32[4,512,1]{1,0,2:T(4,128)S(1)}, f32[4,512,1]{1,0,2:T(4,128)}, f32[4,512,128]{2,1,0:T(8,128)S(1)}) %tuple.61, (pred[64,128]{1,0:T(8,128)(4,1)S(1)}, ...), branch_computations={%region_9.9_spmd, %region_10.12_spmd} | conditional | flops 137107456 | bytes 6561824 | solution.py:117
  103.7 1.4 %fusion.26 = (f32[4,512]{1,0:T(4,128)S(1)}, f32[4,512,128]{1,2,0:T(8,128)S(1)}) fusion(bf16[128,4,128]{2,0,1:T(8,128)(2,1)S(1)} %get-tuple-element.115, bf16[2,4,512,128]{3,2,1,0:T(8,128)(2,1)} %get-tuple-element.114, pred[512,128]{0,1:T(8,128)(4,1)S(1)} %copy.20), kind=kOutput, calls=%fused_computation.67 | convolution fusion | flops 67893248 | bytes 1777664 | tf_op jit(solution)/shard_map/while/body/eval_jaxpr/cond/branch_1_fun/hqd,khd->hqk/dot_general | solution.py:36
  105.3 1.3 %bitcast_add_fusion.1 = f32[4,512,1]{1,0,2:T(4,128)} fusion(f32[4,512]{1,0:T(4,128)S(1)} %fusion.13, f32[4,512,1]{1,0,2:T(4,128)} %get-tuple-element.116, f32[4,512,1]{1,0,2:T(4,128)S(1)} %get-tuple-element.112, f32[4,512,1]{1,0,2:T(4,128)S(1)} %get-tuple-element.356), kind=kLoop, calls=%fused_computation.28 | loop fusion | flops 6144 | bytes 40960 | tf_op jit(solution)/shard_map/while/body/eval_jaxpr/cond/branch_1_fun/add | solution.py:44
  112.1 1.4 %fusion.32 = (pred[]{:T(512)}, pred[64,128]{1,0:T(8,128)(4,1)S(1)}, pred[]{:T(512)}, pred[64,128]{1,0:T(8,128)(4,1)}) fusion(s32[64]{0:T(128)S(1)} %get-tuple-element.331, s32[128]{0:T(128)S(1)} %dynamic_slice.38, s32[64]{0:T(128)S(1)} %get-tuple-element.332, s32[128]{0:T(128)S(1)} %dynamic_slice.39, s32[64]{0:T(128)S(1)} %get-tuple-element.333, ...), kind=kLoop, calls=%fused_computation.64.clone.1 | loop fusion | flops 65534 | bytes 18434 | tf_op jit(solution)/shard_map/while/body/eval_jaxpr/reduce_or | solution.py:118
  115.0 1.4 %divide_convert_fusion = (bf16[4,512,128]{2,1,0:T(8,128)(2,1)S(1)}, bf16[4,512,128]{2,1,0:T(8,128)(2,1)S(1)}) fusion(f32[4,512,128]{2,1,0:T(8,128)S(1)} %get-tuple-element.146, f32[4,512]{1,0:T(4,128)} %bitcast.31, f32[4,512,128]{2,1,0:T(8,128)S(1)} %get-tuple-element.144, f32[4,512]{1,0:T(4,128)} %bitcast.105), kind=kLoop, calls=%fused_computation.46 | loop fusion | flops 1048576 | bytes 3162112 | tf_op jit(solution)/shard_map/convert.4
  (107 shorter events, 31.9 us)
Async XLA Ops:
  6.5 62.6 %all-gather.2.cloned.1.call-start = ((), (), s32[]{:S(2)}) async-start(), calls=%async_computation | async-start | bytes 1310720 | tf_op jit(solution)/shard_map/all_gather | solution.py:99
  6.5 29.5 %collective-permute-start = (bf16[128,5120]{1,0:T(8,128)(2,1)}, bf16[128,5120]{1,0:T(8,128)(2,1)S(1)}, u32[]{:S(2)}, u32[]{:S(2)}) collective-permute-start(bf16[128,5120]{1,0:T(8,128)(2,1)} %bitcast.102), channel_id=1, source_target_pairs={{0,4},{4,8},{8,12},{12,16},{16,20},{20,24},{24,28},{28,0},{1,5},{5... | collective-permute-start | bytes 3932168 | tf_op jit(solution)/shard_map/ppermute | solution.py:17
  9.2 30.8 %collective-permute-start.1 = (bf16[128,5120]{1,0:T(8,128)(2,1)}, bf16[128,5120]{1,0:T(8,128)(2,1)}, u32[]{:S(2)}, u32[]{:S(2)}) collective-permute-start(bf16[128,5120]{1,0:T(8,128)(2,1)} %bitcast.103), channel_id=1, source_target_pairs={{0,28},{4,0},{8,4},{12,8},{16,12},{20,16},{24,20},{28,24},{1,29},{... | collective-permute-start | bytes 3932168 | tf_op jit(solution)/shard_map/ppermute | solution.py:17
  12.5 30.2 %copy-start.2 = (s32[1,8]{1,0:T(1,128)S(1)}, s32[1,8]{1,0:T(1,128)}, u32[]{:S(2)}) copy-start(s32[1,8]{1,0:T(1,128)} %param.11) | copy-start | bytes 100
  84.5 1.6 %copy-start = (f32[4,512,1]{1,0,2:T(4,128)S(1)}, f32[4,512,1]{1,0,2:T(4,128)}, u32[]{:S(2)}) copy-start(f32[4,512,1]{1,0,2:T(4,128)} %get-tuple-element.109) | copy-start | bytes 24580 | tf_op jit(solution)/shard_map/while/body/eval_jaxpr/cond
  86.1 0.7 copy-start.1
  94.8 1.6 %copy-start = (f32[4,512,1]{1,0,2:T(4,128)S(1)}, f32[4,512,1]{1,0,2:T(4,128)}, u32[]{:S(2)}) copy-start(f32[4,512,1]{1,0,2:T(4,128)} %get-tuple-element.109) | copy-start | bytes 24580 | tf_op jit(solution)/shard_map/while/body/eval_jaxpr/cond
  96.4 0.7 copy-start.1
Sparse Core Ops, SparseCore 0:
  42.9 26.1 all-gather.1
where the time goes:
time: 126 us; the launch traced here: 125 us
  waiting for transfers between devices  47.9 us (38%)
  local copies, waits for them, and re-layouts  28.8 us (23%)
  other arithmetic  16.2 us (13%)
  between operations  13.5 us (11%)
  matrix products  8.41 us (7%)
  loops' own time  8.04 us (6%)
  starting transfers between devices  2.68 us (2%)
    ppermute x2, waiting for transfers between devices, passed_along(): lax.ppermute(array, axis, [(i, (i + by) % devices) for i in range(devices)])  27.5 us
    all_gather x1, waiting for transfers between devices, on_device(): portion = lax.all_gather(key_values, 'ctx', axis=0, tiled=True)  20.3 us
    another operation x1, loops' own time, on_device(): lax.scan(absorb_block, (fresh_state(), fresh_state()), (block_list, jnp.a...  7.71 us
    reduce_or x4, other arithmetic, absorb_block(): jnp.any(visible)  5.6 us
    dot_general x4, matrix products, attend(): jnp.einsum('hqd,khd->hqk', query_head_rows, key_rows, preferred_element_t...  5.54 us
    dynamic_slice x12, local copies, waits for them, and re-layouts, on_device(): lax.scan(absorb_block, (fresh_state(), fresh_state()), (block_list, jnp.a...  5.37 us
    dynamic_slice x4, local copies, waits for them, and re-layouts, absorb_block(): key_positions = lax.dynamic_slice_in_dim(positions, first_row, local_rows)  3 us
    le x4, local copies, waits for them, and re-layouts, absorb_block(): key_positions[None, :] <= own_positions[half_index][:, None]  2.99 us
  transfers between devices with their start and end apart: 3, of which 3 were waited for; matrix products, arithmetic and copies ran while one was open for 7% of the time, Pallas kernels for 0%

commit v1 on v0

--- a/solution.py
+++ b/solution.py
@@ -96,7 +96,12 @@
             jnp.zeros((KEY_VALUE_HEADS, QUERIES_PER_KV * exchanged_rows, HEAD_SIZE), jnp.float32),
         )
 
-    portion = lax.all_gather(key_values, "ctx", axis=0, tiled=True)
+    ring = [key_values]
+    for hop in range(3):
+        ring.append(lax.ppermute(ring[-1], "ctx", [(dev, (dev + 1) % 4) for dev in range(4)]))
+    portion = jnp.roll(
+        jnp.concatenate(ring[::-1], axis=0), (lax.axis_index("ctx") + 1) * ring[0].shape[0], axis=0
+    )
     piece_rows = portion.shape[0]
     count_of_blocks = piece_rows // local_rows
     block_list = portion.reshape(count_of_blocks, local_rows, 2, KEY_VALUE_HEADS, HEAD_SIZE)

time: 126 us -> 111 us (0.88)
  between operations: 13.5 us -> 0.22 us
  waiting for transfers between devices: 47.9 us -> 42.9 us
  starting transfers between devices: 2.68 us -> 5.31 us
  local copies, waits for them, and re-layouts: 28.8 us -> 27 us
    all_gather x1 -> x0, waiting for transfers between devices: 20.3 us -> none  [on_device(): portion = lax.all_gather(key_values, 'ctx', axis=0, tiled=True)]
    ppermute x0 -> x3, waiting for transfers between devices: none -> 15.8 us  [on_device(): lax.ppermute(ring[-1], 'ctx', [(dev, (dev + 1) % 4) for dev in range(4)])]
    ppermute x0 -> x3, starting transfers between devices: none -> 2.63 us  [on_device(): lax.ppermute(ring[-1], 'ctx', [(dev, (dev + 1) % 4) for dev in range(4)])]
  transfers between devices with their start and end apart: 3 -> 5, of which waited for: 3 -> 5; matrix products, arithmetic and copies ran while one was open for 7% -> 10% of each run, Pallas kernels for 0% -> 0%
where the time goes in v1:
time: 111 us; the launch traced here: 109 us
  waiting for transfers between devices  42.9 us (39%)
  local copies, waits for them, and re-layouts  27 us (24%)
  other arithmetic  17.4 us (16%)
  matrix products  8.42 us (8%)
  loops' own time  8.01 us (7%)
  starting transfers between devices  5.31 us (5%)
    ppermute x2, waiting for transfers between devices, passed_along(): lax.ppermute(array, axis, [(i, (i + by) % devices) for i in range(devices)])  27.1 us
    ppermute x3, waiting for transfers between devices, on_device(): lax.ppermute(ring[-1], 'ctx', [(dev, (dev + 1) % 4) for dev in range(4)])  15.8 us
    another operation x1, loops' own time, on_device(): lax.scan(absorb_block, (fresh_state(), fresh_state()), (block_list, jnp.a...  7.69 us
    reduce_or x4, other arithmetic, absorb_block(): jnp.any(visible)  5.57 us
    dot_general x4, matrix products, attend(): jnp.einsum('hqd,khd->hqk', query_head_rows, key_rows, preferred_element_t...  5.55 us
    dynamic_slice x12, local copies, waits for them, and re-layouts, on_device(): lax.scan(absorb_block, (fresh_state(), fresh_state()), (block_list, jnp.a...  5.22 us
    le x4, local copies, waits for them, and re-layouts, absorb_block(): key_positions[None, :] <= own_positions[half_index][:, None]  3.05 us
    dynamic_slice x4, local copies, waits for them, and re-layouts, absorb_block(): key_documents = lax.dynamic_slice_in_dim(documents, first_row, local_rows)  2.95 us
  transfers between devices with their start and end apart: 5, of which 5 were waited for; matrix products, arithmetic and copies ran while one was open for 10% of the time, Pallas kernels for 0%

profile of v1, /device:TPU:1, one launch (start us, length us, event | category | flops | bytes accessed | tf_op | source)
XLA Modules:
  0.0 109.2 jit_solution(6835966499299586308)
XLA Ops:
  0.0 2.7 %collective-permute-start = (bf16[128,5120]{1,0:T(8,128)(2,1)}, bf16[128,5120]{1,0:T(8,128)(2,1)S(1)}, u32[]{:S(2)}, u32[]{:S(2)}) collective-permute-start(bf16[128,5120]{1,0:T(8,128)(2,1)} %bitcast.102), channel_id=1, source_target_pairs={{0,4},{4,8},{8,12},{12,16},{16,20},{20,24},{24,28},{28,0},{1,5},{5... | collective-permute-start | bytes 3932168 | tf_op jit(solution)/shard_map/ppermute | solution.py:17
  6.4 23.1 %collective-permute-done = bf16[128,5120]{1,0:T(8,128)(2,1)S(1)} collective-permute-done((bf16[128,5120]{1,0:T(8,128)(2,1)}, bf16[128,5120]{1,0:T(8,128)(2,1)S(1)}, u32[]{:S(2)}, u32[]{:S(2)}) %collective-permute-start) | collective-permute-done | bytes 1310752 | tf_op jit(solution)/shard_map/ppermute | solution.py:17
  29.5 4.0 %collective-permute-done.1 = bf16[128,5120]{1,0:T(8,128)(2,1)} collective-permute-done((bf16[128,5120]{1,0:T(8,128)(2,1)}, bf16[128,5120]{1,0:T(8,128)(2,1)}, u32[]{:S(2)}, u32[]{:S(2)}) %collective-permute-start.1) | collective-permute-done | bytes 1310752 | tf_op jit(solution)/shard_map/ppermute | solution.py:17
  33.5 2.0 %select_select_fusion = bf16[128,5120]{1,0:T(8,128)(2,1)S(1)} fusion(bf16[128,5120]{1,0:T(8,128)(2,1)S(1)} %collective-permute-done, bf16[128,5120]{1,0:T(8,128)(2,1)} %collective-permute-done.1, pred[128]{0:T(512)(128)(4,1)S(1)} %eq.77, pred[128]{0:T(512)(128)(4,1)S(1)} %eq.73, bf16[1,128,5120]{2,1,0:T(8,128)(2,1)} %param.10), kind=kLoop, calls=%fused_computation.43 | loop fusion | flops 1310720 | bytes 5243136 | tf_op jit(solution)/shard_map/jit(_where)/select_n | solution.py:72
  35.5 1.8 %collective-permute-start.2 = (bf16[128,1024]{1,0:T(8,128)(2,1)S(1)}, bf16[128,1024]{1,0:T(8,128)(2,1)S(1)}, u32[]{:S(2)}, u32[]{:S(2)}) collective-permute-start(bf16[128,1024]{1,0:T(8,128)(2,1)S(1)} %slice.38), channel_id=1, source_target_pairs={{0,1},{1,2},{2,3},{3,0},{4,5},{5,6},{6,7},{7,4},{8,9},{9,10},{10,1... | collective-permute-start | bytes 786440 | tf_op jit(solution)/shard_map/ppermute | solution.py:101
  38.1 5.4 %collective-permute-done.2 = bf16[128,1024]{1,0:T(8,128)(2,1)S(1)} collective-permute-done((bf16[128,1024]{1,0:T(8,128)(2,1)S(1)}, bf16[128,1024]{1,0:T(8,128)(2,1)S(1)}, u32[]{:S(2)}, u32[]{:S(2)}) %collective-permute-start.2) | collective-permute-done | bytes 262176 | tf_op jit(solution)/shard_map/ppermute | solution.py:101
  48.5 3.9 %collective-permute-done.3 = bf16[128,1024]{1,0:T(8,128)(2,1)S(1)} collective-permute-done((bf16[128,1024]{1,0:T(8,128)(2,1)S(1)}, bf16[128,1024]{1,0:T(8,128)(2,1)S(1)}, u32[]{:S(2)}, u32[]{:S(2)}) %collective-permute-start.3) | collective-permute-done | bytes 262176 | tf_op jit(solution)/shard_map/ppermute | solution.py:101
  52.8 1.4 %copy.22 = bf16[2,64,4,8,128]{4,1,3,2,0:T(8,128)(2,1)} copy(bf16[2,64,4,8,128]{4,3,2,1,0:T(8,128)(2,1)S(1)} %bitcast.97) | data formatting | bytes 2097152 | tf_op jit(solution)/shard_map/reshape | solution.py:83
  54.2 6.6 %collective-permute-done.4 = bf16[128,1024]{1,0:T(8,128)(2,1)S(1)} collective-permute-done((bf16[128,1024]{1,0:T(8,128)(2,1)S(1)}, bf16[128,1024]{1,0:T(8,128)(2,1)S(1)}, u32[]{:S(2)}, u32[]{:S(2)}) %collective-permute-start.4) | collective-permute-done | bytes 262176 | tf_op jit(solution)/shard_map/ppermute | solution.py:101
  63.7 41.9 %while.20 = (s32[]{:T(128)}, f32[4,512,1]{1,0,2:T(4,128)S(1)}, f32[4,512,1]{1,0,2:T(4,128)}, f32[4,512,128]{2,1,0:T(8,128)S(1)}, f32[4,512,1]{1,0,2:T(4,128)S(1)...) while((s32[]{:T(128)}, f32[4,512,1]{1,0,2:T(4,128)S(1)}, ...), condition=%wide.region_13.14_spmd, body=%wide.region_2.13_spmd.sunk | while | flops 274280448 | bytes 14785039 | solution.py:135
  67.6 1.4 %fusion.32 = (pred[]{:T(512)}, pred[64,128]{1,0:T(8,128)(4,1)S(1)}, pred[]{:T(512)}, pred[64,128]{1,0:T(8,128)(4,1)}) fusion(s32[64]{0:T(128)S(1)} %get-tuple-element.331, s32[128]{0:T(128)S(1)} %dynamic_slice.44, s32[64]{0:T(128)S(1)} %get-tuple-element.332, s32[128]{0:T(128)S(1)} %dynamic_slice.45, s32[64]{0:T(128)S(1)} %get-tuple-element.333, ...), kind=kLoop, calls=%fused_computation.73.clone.1 | loop fusion | flops 65534 | bytes 18434 | tf_op jit(solution)/shard_map/while/body/eval_jaxpr/reduce_or | solution.py:123
  69.8 3.9 %conditional.5 = ((f32[4,512,1]{1,0,2:T(4,128)S(1)}, f32[4,512,1]{1,0,2:T(4,128)}, f32[4,512,128]{2,1,0:T(8,128)S(1)})) conditional(s32[]{:T(128)} %convert_element_type.33, (f32[4,512,1]{1,0,2:T(4,128)S(1)}, f32[4,512,1]{1,0,2:T(4,128)}, f32[4,512,128]{2,1,0:T(8,128)S(1)}) %tuple.61, (pred[64,128]{1,0:T(8,128)(4,1)S(1)}, ...), branch_computations={%region_9.9_spmd, %region_10.12_spmd} | conditional | flops 137107456 | bytes 6561824 | solution.py:122
  70.0 1.4 %fusion.26 = (f32[4,512]{1,0:T(4,128)S(1)}, f32[4,512,128]{1,2,0:T(8,128)S(1)}) fusion(bf16[128,4,128]{2,0,1:T(8,128)(2,1)S(1)} %get-tuple-element.115, bf16[2,4,512,128]{3,2,1,0:T(8,128)(2,1)} %get-tuple-element.114, pred[512,128]{0,1:T(8,128)(4,1)S(1)} %copy.20), kind=kOutput, calls=%fused_computation.76 | convolution fusion | flops 67893248 | bytes 1777664 | tf_op jit(solution)/shard_map/while/body/eval_jaxpr/cond/branch_1_fun/hqd,khd->hqk/dot_general | solution.py:36
  71.7 1.3 %bitcast_add_fusion.1 = f32[4,512,1]{1,0,2:T(4,128)} fusion(f32[4,512]{1,0:T(4,128)S(1)} %fusion.13, f32[4,512,1]{1,0,2:T(4,128)} %get-tuple-element.116, f32[4,512,1]{1,0,2:T(4,128)S(1)} %get-tuple-element.112, f32[4,512,1]{1,0,2:T(4,128)S(1)} %get-tuple-element.356), kind=kLoop, calls=%fused_computation.28 | loop fusion | flops 6144 | bytes 40960 | tf_op jit(solution)/shard_map/while/body/eval_jaxpr/cond/branch_1_fun/add | solution.py:44
  74.4 3.3 %conditional.4 = ((f32[4,512,1]{1,0,2:T(4,128)S(1)}, f32[4,512,1]{1,0,2:T(4,128)}, f32[4,512,128]{2,1,0:T(8,128)S(1)})) conditional(s32[]{:T(128)} %convert_element_type.32, (f32[4,512,1]{1,0,2:T(4,128)S(1)}, f32[4,512,1]{1,0,2:T(4,128)}, f32[4,512,128]{2,1,0:T(8,128)S(1)}) %tuple.59, (pred[64,128]{1,0:T(8,128)(4,1)}, ...), branch_computations={%region_4.4_spmd, %region_5.7_spmd} | conditional | flops 137107456 | bytes 6627416 | solution.py:122
  75.3 1.4 %fusion.25 = (f32[4,512]{1,0:T(4,128)S(1)}, f32[4,512,128]{1,2,0:T(8,128)S(1)}) fusion(bf16[128,4,128]{2,0,1:T(8,128)(2,1)S(1)} %get-tuple-element.108, bf16[2,4,512,128]{3,2,1,0:T(8,128)(2,1)} %get-tuple-element.107, pred[512,128]{0,1:T(8,128)(4,1)S(1)} %copy.18), kind=kOutput, calls=%fused_computation.75 | convolution fusion | flops 67893248 | bytes 1777664 | tf_op jit(solution)/shard_map/while/body/eval_jaxpr/cond/branch_1_fun/hqd,khd->hqk/dot_general | solution.py:36
  81.7 1.4 %fusion.32 = (pred[]{:T(512)}, pred[64,128]{1,0:T(8,128)(4,1)S(1)}, pred[]{:T(512)}, pred[64,128]{1,0:T(8,128)(4,1)}) fusion(s32[64]{0:T(128)S(1)} %get-tuple-element.331, s32[128]{0:T(128)S(1)} %dynamic_slice.44, s32[64]{0:T(128)S(1)} %get-tuple-element.332, s32[128]{0:T(128)S(1)} %dynamic_slice.45, s32[64]{0:T(128)S(1)} %get-tuple-element.333, ...), kind=kLoop, calls=%fused_computation.73.clone.1 | loop fusion | flops 65534 | bytes 18434 | tf_op jit(solution)/shard_map/while/body/eval_jaxpr/reduce_or | solution.py:123
  84.6 3.3 %conditional.4 = ((f32[4,512,1]{1,0,2:T(4,128)S(1)}, f32[4,512,1]{1,0,2:T(4,128)}, f32[4,512,128]{2,1,0:T(8,128)S(1)})) conditional(s32[]{:T(128)} %convert_element_type.32, (f32[4,512,1]{1,0,2:T(4,128)S(1)}, f32[4,512,1]{1,0,2:T(4,128)}, f32[4,512,128]{2,1,0:T(8,128)S(1)}) %tuple.59, (pred[64,128]{1,0:T(8,128)(4,1)}, ...), branch_computations={%region_4.4_spmd, %region_5.7_spmd} | conditional | flops 137107456 | bytes 6627416 | solution.py:122
  85.5 1.4 %fusion.25 = (f32[4,512]{1,0:T(4,128)S(1)}, f32[4,512,128]{1,2,0:T(8,128)S(1)}) fusion(bf16[128,4,128]{2,0,1:T(8,128)(2,1)S(1)} %get-tuple-element.108, bf16[2,4,512,128]{3,2,1,0:T(8,128)(2,1)} %get-tuple-element.107, pred[512,128]{0,1:T(8,128)(4,1)S(1)} %copy.18), kind=kOutput, calls=%fused_computation.75 | convolution fusion | flops 67893248 | bytes 1777664 | tf_op jit(solution)/shard_map/while/body/eval_jaxpr/cond/branch_1_fun/hqd,khd->hqk/dot_general | solution.py:36
  91.9 1.4 %fusion.32 = (pred[]{:T(512)}, pred[64,128]{1,0:T(8,128)(4,1)S(1)}, pred[]{:T(512)}, pred[64,128]{1,0:T(8,128)(4,1)}) fusion(s32[64]{0:T(128)S(1)} %get-tuple-element.331, s32[128]{0:T(128)S(1)} %dynamic_slice.44, s32[64]{0:T(128)S(1)} %get-tuple-element.332, s32[128]{0:T(128)S(1)} %dynamic_slice.45, s32[64]{0:T(128)S(1)} %get-tuple-element.333, ...), kind=kLoop, calls=%fused_computation.73.clone.1 | loop fusion | flops 65534 | bytes 18434 | tf_op jit(solution)/shard_map/while/body/eval_jaxpr/reduce_or | solution.py:123
  94.1 3.9 %conditional.5 = ((f32[4,512,1]{1,0,2:T(4,128)S(1)}, f32[4,512,1]{1,0,2:T(4,128)}, f32[4,512,128]{2,1,0:T(8,128)S(1)})) conditional(s32[]{:T(128)} %convert_element_type.33, (f32[4,512,1]{1,0,2:T(4,128)S(1)}, f32[4,512,1]{1,0,2:T(4,128)}, f32[4,512,128]{2,1,0:T(8,128)S(1)}) %tuple.61, (pred[64,128]{1,0:T(8,128)(4,1)S(1)}, ...), branch_computations={%region_9.9_spmd, %region_10.12_spmd} | conditional | flops 137107456 | bytes 6561824 | solution.py:122
  94.3 1.4 %fusion.26 = (f32[4,512]{1,0:T(4,128)S(1)}, f32[4,512,128]{1,2,0:T(8,128)S(1)}) fusion(bf16[128,4,128]{2,0,1:T(8,128)(2,1)S(1)} %get-tuple-element.115, bf16[2,4,512,128]{3,2,1,0:T(8,128)(2,1)} %get-tuple-element.114, pred[512,128]{0,1:T(8,128)(4,1)S(1)} %copy.20), kind=kOutput, calls=%fused_computation.76 | convolution fusion | flops 67893248 | bytes 1777664 | tf_op jit(solution)/shard_map/while/body/eval_jaxpr/cond/branch_1_fun/hqd,khd->hqk/dot_general | solution.py:36
  102.7 1.4 %fusion.32 = (pred[]{:T(512)}, pred[64,128]{1,0:T(8,128)(4,1)S(1)}, pred[]{:T(512)}, pred[64,128]{1,0:T(8,128)(4,1)}) fusion(s32[64]{0:T(128)S(1)} %get-tuple-element.331, s32[128]{0:T(128)S(1)} %dynamic_slice.44, s32[64]{0:T(128)S(1)} %get-tuple-element.332, s32[128]{0:T(128)S(1)} %dynamic_slice.45, s32[64]{0:T(128)S(1)} %get-tuple-element.333, ...), kind=kLoop, calls=%fused_computation.73.clone.1 | loop fusion | flops 65534 | bytes 18434 | tf_op jit(solution)/shard_map/while/body/eval_jaxpr/reduce_or | solution.py:123
  105.6 1.4 %divide_convert_fusion = (bf16[4,512,128]{2,1,0:T(8,128)(2,1)S(1)}, bf16[4,512,128]{2,1,0:T(8,128)(2,1)S(1)}) fusion(f32[4,512,128]{2,1,0:T(8,128)S(1)} %get-tuple-element.146, f32[4,512]{1,0:T(4,128)} %bitcast.31, f32[4,512,128]{2,1,0:T(8,128)S(1)} %get-tuple-element.144, f32[4,512]{1,0:T(4,128)} %bitcast.105), kind=kLoop, calls=%fused_computation.46 | loop fusion | flops 1048576 | bytes 3162112 | tf_op jit(solution)/shard_map/convert.4
  (119 shorter events, 36.6 us)
Async XLA Ops:
  0.0 29.5 %collective-permute-start = (bf16[128,5120]{1,0:T(8,128)(2,1)}, bf16[128,5120]{1,0:T(8,128)(2,1)S(1)}, u32[]{:S(2)}, u32[]{:S(2)}) collective-permute-start(bf16[128,5120]{1,0:T(8,128)(2,1)} %bitcast.102), channel_id=1, source_target_pairs={{0,4},{4,8},{8,12},{12,16},{16,20},{20,24},{24,28},{28,0},{1,5},{5... | collective-permute-start | bytes 3932168 | tf_op jit(solution)/shard_map/ppermute | solution.py:17
  2.7 30.8 %collective-permute-start.1 = (bf16[128,5120]{1,0:T(8,128)(2,1)}, bf16[128,5120]{1,0:T(8,128)(2,1)}, u32[]{:S(2)}, u32[]{:S(2)}) collective-permute-start(bf16[128,5120]{1,0:T(8,128)(2,1)} %bitcast.103), channel_id=1, source_target_pairs={{0,28},{4,0},{8,4},{12,8},{16,12},{20,16},{24,20},{28,24},{1,29},{... | collective-permute-start | bytes 3932168 | tf_op jit(solution)/shard_map/ppermute | solution.py:17
  6.4 30.8 %copy-start.2 = (s32[8,8]{1,0:T(8,128)S(1)}, s32[8,8]{1,0:T(8,128)}, u32[]{:S(2)}) copy-start(s32[8,8]{1,0:T(8,128)} %param.13) | copy-start | bytes 772
  35.5 8.0 %collective-permute-start.2 = (bf16[128,1024]{1,0:T(8,128)(2,1)S(1)}, bf16[128,1024]{1,0:T(8,128)(2,1)S(1)}, u32[]{:S(2)}, u32[]{:S(2)}) collective-permute-start(bf16[128,1024]{1,0:T(8,128)(2,1)S(1)} %slice.38), channel_id=1, source_target_pairs={{0,1},{1,2},{2,3},{3,0},{4,5},{5,6},{6,7},{7,4},{8,9},{9,10},{10,1... | collective-permute-start | bytes 786440 | tf_op jit(solution)/shard_map/ppermute | solution.py:101
  43.5 8.9 %collective-permute-start.3 = (bf16[128,1024]{1,0:T(8,128)(2,1)S(1)}, bf16[128,1024]{1,0:T(8,128)(2,1)S(1)}, u32[]{:S(2)}, u32[]{:S(2)}) collective-permute-start(bf16[128,1024]{1,0:T(8,128)(2,1)S(1)} %collective-permute-done.2), channel_id=1, source_target_pairs={{0,1},{1,2},{2,3},{3,0},{4,5},{5,6},{6,7},{7,4},{8,9},{9,10},{10,1... | collective-permute-start | bytes 786440 | tf_op jit(solution)/shard_map/ppermute | solution.py:101
  52.4 8.4 %collective-permute-start.4 = (bf16[128,1024]{1,0:T(8,128)(2,1)S(1)}, bf16[128,1024]{1,0:T(8,128)(2,1)S(1)}, u32[]{:S(2)}, u32[]{:S(2)}) collective-permute-start(bf16[128,1024]{1,0:T(8,128)(2,1)S(1)} %collective-permute-done.3), channel_id=1, source_target_pairs={{0,1},{1,2},{2,3},{3,0},{4,5},{5,6},{6,7},{7,4},{8,9},{9,10},{10,1... | collective-permute-start | bytes 786440 | tf_op jit(solution)/shard_map/ppermute | solution.py:101
  75.3 1.6 %copy-start = (f32[4,512,1]{1,0,2:T(4,128)S(1)}, f32[4,512,1]{1,0,2:T(4,128)}, u32[]{:S(2)}) copy-start(f32[4,512,1]{1,0,2:T(4,128)} %get-tuple-element.109) | copy-start | bytes 24580 | tf_op jit(solution)/shard_map/while/body/eval_jaxpr/cond
  76.9 0.8 copy-start.1
  85.5 1.7 %copy-start = (f32[4,512,1]{1,0,2:T(4,128)S(1)}, f32[4,512,1]{1,0,2:T(4,128)}, u32[]{:S(2)}) copy-start(f32[4,512,1]{1,0,2:T(4,128)} %get-tuple-element.109) | copy-start | bytes 24580 | tf_op jit(solution)/shard_map/while/body/eval_jaxpr/cond
  87.2 0.8 copy-start.1
